TPU v7x, 32 devices: a whole 2x2x4 slice. The times are simulated.
32 devices in a mesh: head: 4 (over z), outer: 2 (over core), inner: 4 (over y, x).
Axes of the slice: x: 2, y: 2, z: 4, core: 2. Of those that a mesh axis runs over, the one named last changes fastest.
Arguments:
- query: bfloat16 [4096, 8192], P(('outer', 'inner', 'head')), may hold values from -100 to 100
- keys: bfloat16 [4096, 1024], P(('outer', 'inner', 'head')), may hold values from -4.5 to 4.5
- values: bfloat16 [4096, 1024], P(('outer', 'inner', 'head')), may hold values from -6 to 6
- lengths: int32 [8], replicated, may hold values from 1 to 1024, 4096 in all
Outputs:
- attended: bfloat16 [4096, 8192], P(('outer', 'inner', 'head'))
Inputs may be any that keep to these rules, and one draw needn't show every extreme that they name: `lengths`: they sum to 4096, and the longest is exactly 1024.
All inputs are finite; a program needn't handle non-finite values.
Results may differ from a plain program's by a relative error of at most 0.0038.
Values may be sent and summed in bfloat16 or wider, within the bound.
A program may use at most 64 MiB of HBM per device.

v0:
```python
import math
import jax
import jax.numpy as jnp
from jax import lax
from jax.sharding import PartitionSpec as P

HEAD_SIZE = 128


def from_behind(value, axis, steps):
    count = lax.axis_size(axis)
    leading, last = (max(0, -steps), min(count, count - steps))
    return lax.ppermute(value, axis, [(source, source + steps) for source in range(leading, last)])


def doc_numbers(lengths, start_pos, count):
    ends = jnp.cumsum(lengths)
    positions = start_pos + lax.iota(jnp.int32, count)
    numbers = jnp.sum((positions[:, None] >= ends[None, :]).astype(jnp.int32), axis=1)
    return (numbers, positions)


def per_device(query, keys, values, lengths):
    query_local, keys_local, values_local = (
        lax.all_to_all(query, "head", split_axis=1, concat_axis=0, tiled=True),
        lax.all_to_all(keys, "head", split_axis=1, concat_axis=0, tiled=True),
        lax.all_to_all(values, "head", split_axis=1, concat_axis=0, tiled=True),
    )
    local_len = query_local.shape[0]
    pair_heads = keys_local.shape[1] // HEAD_SIZE
    group_width = query_local.shape[1] // keys_local.shape[1]
    context_count = lax.axis_size(("outer", "inner"))
    reach_hops = min(2, context_count // 4)
    position_index = lax.axis_index(("outer", "inner"))
    query_docs, query_pos = doc_numbers(lengths, position_index * local_len, local_len)
    query_groups = jnp.transpose(
        query_local.reshape(local_len, pair_heads, group_width, HEAD_SIZE), (2, 0, 1, 3)
    )
    score_scale = 1.0 / math.sqrt(HEAD_SIZE)

    def attend(state, stacked, distance):
        key_heads = stacked[0].reshape(local_len, pair_heads, HEAD_SIZE)
        value_heads = stacked[1].reshape(local_len, pair_heads, HEAD_SIZE)
        key_docs, key_pos = doc_numbers(lengths, (position_index - distance) * local_len, local_len)
        visible = (
            (query_docs[:, None] == key_docs[None, :])
            & (key_pos[None, :] <= query_pos[:, None])
            & (key_pos[None, :] >= 0)
        )

        def one_group(operands):
            query_part, running_max, running_total, running_sum = operands
            scores = (
                jnp.einsum(
                    "qkd,ckd->kqc", query_part, key_heads, preferred_element_type=jnp.float32
                )
                * score_scale
            )
            masked = jnp.where(visible, scores, -1e30)
            new_max = jnp.maximum(running_max, jnp.max(masked, axis=2))
            weights = jnp.where(visible, jnp.exp(masked - new_max[..., None]), 0.0)
            shrink = jnp.exp(running_max - new_max)
            new_total = running_total * shrink + jnp.sum(weights, axis=2)
            update = jnp.einsum(
                "kqc,ckd->qkd",
                weights.astype(jnp.bfloat16),
                value_heads,
                preferred_element_type=jnp.float32,
            )
            new_sum = running_sum * jnp.transpose(shrink, (1, 0))[..., None] + update
            return (new_max, new_total, new_sum)

        return lax.map(one_group, (query_groups, state[0], state[1], state[2]))

    start_state = (
        jnp.full((group_width, pair_heads, local_len), -1e30, jnp.float32),
        jnp.zeros((group_width, pair_heads, local_len), jnp.float32),
        jnp.zeros((group_width, local_len, pair_heads, HEAD_SIZE), jnp.float32),
    )
    own_pair = jnp.stack((keys_local, values_local))
    state = attend(start_state, own_pair, 0)
    carried = own_pair
    for distance in range(1, reach_hops + 1):
        carried = from_behind(carried, ("outer", "inner"), 1)
        state = attend(state, carried, distance)
    running_max, running_total, running_sum = state
    outcome = running_sum / jnp.transpose(running_total, (0, 2, 1))[..., None]
    outcome = jnp.transpose(outcome, (1, 2, 0, 3))
    outcome = outcome.reshape(local_len, pair_heads * group_width * HEAD_SIZE).astype(jnp.bfloat16)
    return lax.all_to_all(outcome, "head", split_axis=0, concat_axis=1, tiled=True)


def solution(mesh):
    placed = (
        P(("outer", "inner", "head"), None),
        P(("outer", "inner", "head"), None),
        P(("outer", "inner", "head"), None),
        P(),
    )
    return jax.shard_map(
        per_device,
        mesh=mesh,
        in_specs=placed,
        out_specs=P(("outer", "inner", "head"), None),
        check_vma=False,
    )
```

profile of v0, /device:TPU:0, one launch (start us, length us, event | category | flops | bytes accessed | tf_op | source)
XLA Modules:
  0.0 246.9 jit_solution(3934203246122695590)
XLA Ops:
  0.0 1.9 copy.56
  1.9 6.3 %all-to-all-start.1 = ((bf16[128,4,256]{0,2,1:T(8,128)(2,1)}), bf16[128,4,256]{0,2,1:T(8,128)(2,1)S(1)}, u32[]{:S(2)}, u32[]{:S(2)}) async-start(bf16[128,4,256]{0,2,1:T(8,128)(2,1)} %bitcast.2), calls=%async_computation.1 | async-start | bytes 524288 | tf_op jit(solution)/shard_map/all_to_all | solution.py:26
  8.3 1.8 copy.58
  10.1 7.1 %all-to-all-done.1 = bf16[128,4,256]{0,2,1:T(8,128)(2,1)S(1)} async-done(((bf16[128,4,256]{0,2,1:T(8,128)(2,1)}), bf16[128,4,256]{0,2,1:T(8,128)(2,1)S(1)}, u32[]{:S(2)}, u32[]{:S(2)}) %all-to-all-start.1) | async-done | bytes 262176 | tf_op jit(solution)/shard_map/all_to_all | solution.py:26
  17.2 3.4 %all-to-all-start.2 = ((bf16[128,4,256]{0,2,1:T(8,128)(2,1)}), bf16[128,4,256]{0,2,1:T(8,128)(2,1)S(1)}, u32[]{:S(2)}, u32[]{:S(2)}) async-start(bf16[128,4,256]{0,2,1:T(8,128)(2,1)} %bitcast.4), calls=%async_computation.2 | async-start | bytes 524288 | tf_op jit(solution)/shard_map/all_to_all | solution.py:27
  22.2 5.4 %all-to-all-done.2 = bf16[128,4,256]{0,2,1:T(8,128)(2,1)S(1)} async-done(((bf16[128,4,256]{0,2,1:T(8,128)(2,1)}), bf16[128,4,256]{0,2,1:T(8,128)(2,1)S(1)}, u32[]{:S(2)}, u32[]{:S(2)}) %all-to-all-start.2) | async-done | bytes 262176 | tf_op jit(solution)/shard_map/all_to_all | solution.py:27
  27.6 3.6 %all-to-all-start = ((bf16[128,4,2048]{2,0,1:T(8,128)(2,1)}), bf16[128,4,2048]{2,0,1:T(8,128)(2,1)S(1)}, u32[]{:S(2)}, u32[]{:S(2)}) async-start(bf16[128,4,2048]{2,0,1:T(8,128)(2,1)} %bitcast.143), calls=%async_computation | async-start | bytes 4194304 | tf_op jit(solution)/shard_map/all_to_all | solution.py:25
  31.6 4.2 %collective-permute-start = (bf16[2,512,256]{2,1,0:T(8,128)(2,1)S(1)}, bf16[2,512,256]{2,1,0:T(8,128)(2,1)}, u32[]{:S(2)}, u32[]{:S(2)}) collective-permute-start(bf16[2,512,256]{2,1,0:T(8,128)(2,1)S(1)} %pad_maximum_fusion), channel_id=1, source_target_pairs={{0,1},{1,2},{2,3},{3,4},{4,5},{5,6},{6,7},{8,9},{9,10},{10,11},{11... | collective-permute-start | bytes 1572872 | tf_op jit(solution)/shard_map/ppermute | solution.py:13
  35.8 7.3 %collective-permute-done = bf16[2,512,256]{2,1,0:T(8,128)(2,1)} collective-permute-done((bf16[2,512,256]{2,1,0:T(8,128)(2,1)S(1)}, bf16[2,512,256]{2,1,0:T(8,128)(2,1)}, u32[]{:S(2)}, u32[]{:S(2)}) %collective-permute-start) | collective-permute-done | bytes 524320 | tf_op jit(solution)/shard_map/ppermute | solution.py:13
  43.2 5.3 %collective-permute-start.1 = (bf16[2,512,256]{2,1,0:T(8,128)(2,1)}, bf16[2,512,256]{2,1,0:T(8,128)(2,1)}, u32[]{:S(2)}, u32[]{:S(2)}) collective-permute-start(bf16[2,512,256]{2,1,0:T(8,128)(2,1)} %collective-permute-done), channel_id=1, source_target_pairs={{0,1},{1,2},{2,3},{3,4},{4,5},{5,6},{6,7},{8,9},{9,10},{10,11},{11... | collective-permute-start | bytes 1572872 | tf_op jit(solution)/shard_map/ppermute | solution.py:13
  52.1 5.0 %collective-permute-done.1 = bf16[2,512,256]{2,1,0:T(8,128)(2,1)} collective-permute-done((bf16[2,512,256]{2,1,0:T(8,128)(2,1)}, bf16[2,512,256]{2,1,0:T(8,128)(2,1)}, u32[]{:S(2)}, u32[]{:S(2)}) %collective-permute-start.1) | collective-permute-done | bytes 524320 | tf_op jit(solution)/shard_map/ppermute | solution.py:13
  58.8 17.9 %all-to-all-done = bf16[128,4,2048]{2,0,1:T(8,128)(2,1)S(1)} async-done(((bf16[128,4,2048]{2,0,1:T(8,128)(2,1)}), bf16[128,4,2048]{2,0,1:T(8,128)(2,1)S(1)}, u32[]{:S(2)}, u32[]{:S(2)}) %all-to-all-start) | async-done | bytes 2097184 | tf_op jit(solution)/shard_map/all_to_all | solution.py:25
  77.8 2.4 broadcast.125.clone.1
  80.3 27.0 %while.43 = (s32[]{:T(128)}, f32[8,2,512]{2,1,0:T(2,128)S(1)}, f32[8,2,512]{2,1,0:T(2,128)S(1)}, f32[8,512,2,128]{3,1,2,0:T(8,128)}, bf16[8,512,2,128]{3,1,2,0:T...) while((s32[]{:T(128)}, f32[8,2,512]{2,1,0:T(2,128)S(1)}, ...), condition=%wide.region_5.6_spmd.clone, body=%wide.region_2.0_spmd.clone.sunk | while | flops 276435968 | bytes 9753745 | solution.py:73
  81.4 1.8 fusion.111
  84.7 1.8 fusion.111
  88.1 1.8 fusion.111
  91.5 1.8 fusion.111
  94.8 1.8 fusion.111
  98.2 1.8 fusion.111
  101.5 1.8 fusion.111
  104.8 1.8 fusion.111
  107.2 2.4 broadcast.125.clone
  109.6 34.8 %while.44 = (s32[]{:T(128)}, f32[8,2,512]{2,1,0:T(2,128)S(1)}, f32[8,2,512]{2,1,0:T(2,128)S(1)}, f32[8,512,2,128]{3,1,2,0:T(8,128)}, f32[8,2,512]{2,1,0:T(2,128)...) while((s32[]{:T(128)}, f32[8,2,512]{2,1,0:T(2,128)S(1)}, ...), condition=%wide.region_10.11_spmd.clone, body=%wide.region_7.10_spmd.clone.sunk | while | flops 276566016 | bytes 9245857 | solution.py:73
  110.6 2.8 %fusion.119 = f32[8,512,2,128]{3,1,2,0:T(8,128)} fusion(f32[8,512,2,128]{3,1,2,0:T(8,128)} %get-tuple-element.807, s32[]{:T(128)} %get-tuple-element.804, bf16[512,2,128]{2,0,1:T(8,128)(2,1)S(1)} %get-tuple-element.829, f32[2,512,512]{1,2,0:T(8,128)S(1)} %get-tuple-element.731, f32[2,512]{1,0:T(2,128)S(1)} %get-tuple-element.733, ...), kind=kOutput, calls=%fused_computation.40.clone.1 | convolution fusion | flops 137101312 | bytes 3678720 | tf_op jit(solution)/shard_map/while/body/eval_jaxpr/kqc,ckd->qkd/dot_general | solution.py:64
  114.9 2.8 %fusion.119 = f32[8,512,2,128]{3,1,2,0:T(8,128)} fusion(f32[8,512,2,128]{3,1,2,0:T(8,128)} %get-tuple-element.807, s32[]{:T(128)} %get-tuple-element.804, bf16[512,2,128]{2,0,1:T(8,128)(2,1)S(1)} %get-tuple-element.829, f32[2,512,512]{1,2,0:T(8,128)S(1)} %get-tuple-element.731, f32[2,512]{1,0:T(2,128)S(1)} %get-tuple-element.733, ...), kind=kOutput, calls=%fused_computation.40.clone.1 | convolution fusion | flops 137101312 | bytes 3678720 | tf_op jit(solution)/shard_map/while/body/eval_jaxpr/kqc,ckd->qkd/dot_general | solution.py:64
  119.2 2.8 %fusion.119 = f32[8,512,2,128]{3,1,2,0:T(8,128)} fusion(f32[8,512,2,128]{3,1,2,0:T(8,128)} %get-tuple-element.807, s32[]{:T(128)} %get-tuple-element.804, bf16[512,2,128]{2,0,1:T(8,128)(2,1)S(1)} %get-tuple-element.829, f32[2,512,512]{1,2,0:T(8,128)S(1)} %get-tuple-element.731, f32[2,512]{1,0:T(2,128)S(1)} %get-tuple-element.733, ...), kind=kOutput, calls=%fused_computation.40.clone.1 | convolution fusion | flops 137101312 | bytes 3678720 | tf_op jit(solution)/shard_map/while/body/eval_jaxpr/kqc,ckd->qkd/dot_general | solution.py:64
  123.6 2.8 %fusion.119 = f32[8,512,2,128]{3,1,2,0:T(8,128)} fusion(f32[8,512,2,128]{3,1,2,0:T(8,128)} %get-tuple-element.807, s32[]{:T(128)} %get-tuple-element.804, bf16[512,2,128]{2,0,1:T(8,128)(2,1)S(1)} %get-tuple-element.829, f32[2,512,512]{1,2,0:T(8,128)S(1)} %get-tuple-element.731, f32[2,512]{1,0:T(2,128)S(1)} %get-tuple-element.733, ...), kind=kOutput, calls=%fused_computation.40.clone.1 | convolution fusion | flops 137101312 | bytes 3678720 | tf_op jit(solution)/shard_map/while/body/eval_jaxpr/kqc,ckd->qkd/dot_general | solution.py:64
  128.0 2.8 %fusion.119 = f32[8,512,2,128]{3,1,2,0:T(8,128)} fusion(f32[8,512,2,128]{3,1,2,0:T(8,128)} %get-tuple-element.807, s32[]{:T(128)} %get-tuple-element.804, bf16[512,2,128]{2,0,1:T(8,128)(2,1)S(1)} %get-tuple-element.829, f32[2,512,512]{1,2,0:T(8,128)S(1)} %get-tuple-element.731, f32[2,512]{1,0:T(2,128)S(1)} %get-tuple-element.733, ...), kind=kOutput, calls=%fused_computation.40.clone.1 | convolution fusion | flops 137101312 | bytes 3678720 | tf_op jit(solution)/shard_map/while/body/eval_jaxpr/kqc,ckd->qkd/dot_general | solution.py:64
  132.3 2.8 %fusion.119 = f32[8,512,2,128]{3,1,2,0:T(8,128)} fusion(f32[8,512,2,128]{3,1,2,0:T(8,128)} %get-tuple-element.807, s32[]{:T(128)} %get-tuple-element.804, bf16[512,2,128]{2,0,1:T(8,128)(2,1)S(1)} %get-tuple-element.829, f32[2,512,512]{1,2,0:T(8,128)S(1)} %get-tuple-element.731, f32[2,512]{1,0:T(2,128)S(1)} %get-tuple-element.733, ...), kind=kOutput, calls=%fused_computation.40.clone.1 | convolution fusion | flops 137101312 | bytes 3678720 | tf_op jit(solution)/shard_map/while/body/eval_jaxpr/kqc,ckd->qkd/dot_general | solution.py:64
  136.6 2.8 %fusion.119 = f32[8,512,2,128]{3,1,2,0:T(8,128)} fusion(f32[8,512,2,128]{3,1,2,0:T(8,128)} %get-tuple-element.807, s32[]{:T(128)} %get-tuple-element.804, bf16[512,2,128]{2,0,1:T(8,128)(2,1)S(1)} %get-tuple-element.829, f32[2,512,512]{1,2,0:T(8,128)S(1)} %get-tuple-element.731, f32[2,512]{1,0:T(2,128)S(1)} %get-tuple-element.733, ...), kind=kOutput, calls=%fused_computation.40.clone.1 | convolution fusion | flops 137101312 | bytes 3678720 | tf_op jit(solution)/shard_map/while/body/eval_jaxpr/kqc,ckd->qkd/dot_general | solution.py:64
  141.0 2.8 %fusion.119 = f32[8,512,2,128]{3,1,2,0:T(8,128)} fusion(f32[8,512,2,128]{3,1,2,0:T(8,128)} %get-tuple-element.807, s32[]{:T(128)} %get-tuple-element.804, bf16[512,2,128]{2,0,1:T(8,128)(2,1)S(1)} %get-tuple-element.829, f32[2,512,512]{1,2,0:T(8,128)S(1)} %get-tuple-element.731, f32[2,512]{1,0:T(2,128)S(1)} %get-tuple-element.733, ...), kind=kOutput, calls=%fused_computation.40.clone.1 | convolution fusion | flops 137101312 | bytes 3678720 | tf_op jit(solution)/shard_map/while/body/eval_jaxpr/kqc,ckd->qkd/dot_general | solution.py:64
  144.4 2.4 broadcast.125
  146.8 34.8 %while.45 = (s32[]{:T(128)}, f32[8,2,512]{2,1,0:T(2,128)S(1)}, f32[8,512,2,128]{3,1,2,0:T(8,128)}, f32[8,2,512]{2,1,0:T(2,128)S(1)}, f32[8,2,512]{2,1,0:T(2,128)...) while((s32[]{:T(128)}, f32[8,2,512]{2,1,0:T(2,128)S(1)}, ...), condition=%wide.region_15.16_spmd.clone, body=%wide.region_12.15_spmd.clone.sunk | while | flops 276566016 | bytes 9241753 | solution.py:73
  147.8 2.8 %fusion.127 = f32[8,512,2,128]{3,1,2,0:T(8,128)} fusion(f32[8,512,2,128]{3,1,2,0:T(8,128)} %get-tuple-element.853, s32[]{:T(128)} %get-tuple-element.851, bf16[512,2,128]{2,0,1:T(8,128)(2,1)S(1)} %get-tuple-element.874, f32[2,512,512]{1,2,0:T(8,128)S(1)} %get-tuple-element.751, f32[2,512]{1,0:T(2,128)S(1)} %get-tuple-element.753, ...), kind=kOutput, calls=%fused_computation.71.clone.1 | convolution fusion | flops 137101312 | bytes 3678720 | tf_op jit(solution)/shard_map/while/body/eval_jaxpr/kqc,ckd->qkd/dot_general | solution.py:64
  152.1 2.8 %fusion.127 = f32[8,512,2,128]{3,1,2,0:T(8,128)} fusion(f32[8,512,2,128]{3,1,2,0:T(8,128)} %get-tuple-element.853, s32[]{:T(128)} %get-tuple-element.851, bf16[512,2,128]{2,0,1:T(8,128)(2,1)S(1)} %get-tuple-element.874, f32[2,512,512]{1,2,0:T(8,128)S(1)} %get-tuple-element.751, f32[2,512]{1,0:T(2,128)S(1)} %get-tuple-element.753, ...), kind=kOutput, calls=%fused_computation.71.clone.1 | convolution fusion | flops 137101312 | bytes 3678720 | tf_op jit(solution)/shard_map/while/body/eval_jaxpr/kqc,ckd->qkd/dot_general | solution.py:64
  156.4 2.8 %fusion.127 = f32[8,512,2,128]{3,1,2,0:T(8,128)} fusion(f32[8,512,2,128]{3,1,2,0:T(8,128)} %get-tuple-element.853, s32[]{:T(128)} %get-tuple-element.851, bf16[512,2,128]{2,0,1:T(8,128)(2,1)S(1)} %get-tuple-element.874, f32[2,512,512]{1,2,0:T(8,128)S(1)} %get-tuple-element.751, f32[2,512]{1,0:T(2,128)S(1)} %get-tuple-element.753, ...), kind=kOutput, calls=%fused_computation.71.clone.1 | convolution fusion | flops 137101312 | bytes 3678720 | tf_op jit(solution)/shard_map/while/body/eval_jaxpr/kqc,ckd->qkd/dot_general | solution.py:64
  160.8 2.8 %fusion.127 = f32[8,512,2,128]{3,1,2,0:T(8,128)} fusion(f32[8,512,2,128]{3,1,2,0:T(8,128)} %get-tuple-element.853, s32[]{:T(128)} %get-tuple-element.851, bf16[512,2,128]{2,0,1:T(8,128)(2,1)S(1)} %get-tuple-element.874, f32[2,512,512]{1,2,0:T(8,128)S(1)} %get-tuple-element.751, f32[2,512]{1,0:T(2,128)S(1)} %get-tuple-element.753, ...), kind=kOutput, calls=%fused_computation.71.clone.1 | convolution fusion | flops 137101312 | bytes 3678720 | tf_op jit(solution)/shard_map/while/body/eval_jaxpr/kqc,ckd->qkd/dot_general | solution.py:64
  165.1 2.8 %fusion.127 = f32[8,512,2,128]{3,1,2,0:T(8,128)} fusion(f32[8,512,2,128]{3,1,2,0:T(8,128)} %get-tuple-element.853, s32[]{:T(128)} %get-tuple-element.851, bf16[512,2,128]{2,0,1:T(8,128)(2,1)S(1)} %get-tuple-element.874, f32[2,512,512]{1,2,0:T(8,128)S(1)} %get-tuple-element.751, f32[2,512]{1,0:T(2,128)S(1)} %get-tuple-element.753, ...), kind=kOutput, calls=%fused_computation.71.clone.1 | convolution fusion | flops 137101312 | bytes 3678720 | tf_op jit(solution)/shard_map/while/body/eval_jaxpr/kqc,ckd->qkd/dot_general | solution.py:64
  169.5 2.9 %fusion.127 = f32[8,512,2,128]{3,1,2,0:T(8,128)} fusion(f32[8,512,2,128]{3,1,2,0:T(8,128)} %get-tuple-element.853, s32[]{:T(128)} %get-tuple-element.851, bf16[512,2,128]{2,0,1:T(8,128)(2,1)S(1)} %get-tuple-element.874, f32[2,512,512]{1,2,0:T(8,128)S(1)} %get-tuple-element.751, f32[2,512]{1,0:T(2,128)S(1)} %get-tuple-element.753, ...), kind=kOutput, calls=%fused_computation.71.clone.1 | convolution fusion | flops 137101312 | bytes 3678720 | tf_op jit(solution)/shard_map/while/body/eval_jaxpr/kqc,ckd->qkd/dot_general | solution.py:64
  173.8 2.8 %fusion.127 = f32[8,512,2,128]{3,1,2,0:T(8,128)} fusion(f32[8,512,2,128]{3,1,2,0:T(8,128)} %get-tuple-element.853, s32[]{:T(128)} %get-tuple-element.851, bf16[512,2,128]{2,0,1:T(8,128)(2,1)S(1)} %get-tuple-element.874, f32[2,512,512]{1,2,0:T(8,128)S(1)} %get-tuple-element.751, f32[2,512]{1,0:T(2,128)S(1)} %get-tuple-element.753, ...), kind=kOutput, calls=%fused_computation.71.clone.1 | convolution fusion | flops 137101312 | bytes 3678720 | tf_op jit(solution)/shard_map/while/body/eval_jaxpr/kqc,ckd->qkd/dot_general | solution.py:64
  178.2 2.8 %fusion.127 = f32[8,512,2,128]{3,1,2,0:T(8,128)} fusion(f32[8,512,2,128]{3,1,2,0:T(8,128)} %get-tuple-element.853, s32[]{:T(128)} %get-tuple-element.851, bf16[512,2,128]{2,0,1:T(8,128)(2,1)S(1)} %get-tuple-element.874, f32[2,512,512]{1,2,0:T(8,128)S(1)} %get-tuple-element.751, f32[2,512]{1,0:T(2,128)S(1)} %get-tuple-element.753, ...), kind=kOutput, calls=%fused_computation.71.clone.1 | convolution fusion | flops 137101312 | bytes 3678720 | tf_op jit(solution)/shard_map/while/body/eval_jaxpr/kqc,ckd->qkd/dot_general | solution.py:64
  181.6 2.9 %fusion.73 = bf16[512,2,8,128]{3,0,1,2:T(8,128)(2,1)S(1)} fusion(f32[8,512,2,128]{3,1,2,0:T(8,128)} %get-tuple-element.167, f32[8,512,2]{1,2,0:T(2,128)S(1)} %bitcast.213), kind=kLoop, calls=%fused_computation.96 | loop fusion | flops 2097152 | bytes 6324224 | tf_op jit(solution)/shard_map/convert_element_type | solution.py:89
  184.5 2.7 %copy.75 = bf16[512,2,8,128]{3,2,1,0:T(8,128)(2,1)} copy(bf16[512,2,8,128]{3,0,1,2:T(8,128)(2,1)S(1)} %fusion.73) | data formatting | bytes 4194304 | tf_op jit(solution)/shard_map/convert_element_type | solution.py:89
  187.1 2.8 %convert_element_type.34 = bf16[4,128,2048]{2,1,0:T(8,128)(2,1)S(1)} reshape(bf16[512,2,8,128]{3,2,1,0:T(8,128)(2,1)} %copy.75) | data formatting | bytes 4194304 | tf_op jit(solution)/shard_map/convert_element_type | solution.py:89
  190.0 51.0 %all_to_all.64 = bf16[4,128,2048]{2,1,0:T(8,128)(2,1)} all-to-all(bf16[4,128,2048]{2,1,0:T(8,128)(2,1)S(1)} %convert_element_type.34), channel_id=1, replica_groups=mesh['head'=4,'outer'=2,'inner'=4] {'head'}, dimensions={0} | all-to-all | bytes 4194304 | tf_op jit(solution)/shard_map/all_to_all | solution.py:90
  241.0 3.0 %copy.76 = bf16[128,4,2048]{0,2,1:T(8,128)(2,1)S(1)} copy(bf16[128,4,2048]{2,0,1:T(8,128)(2,1)} %bitcast.202) | data formatting | bytes 4194304 | tf_op jit(solution)/shard_map/all_to_all | solution.py:90
  244.0 2.9 %copy.77 = bf16[128,8192]{1,0:T(8,128)(2,1)} copy(bf16[128,8192]{0,1:T(8,128)(2,1)S(1)} %bitcast.203) | data formatting | bytes 4194304 | tf_op jit(solution)/shard_map/all_to_all | solution.py:90
  (174 shorter events, 44.0 us)
Async XLA Ops:
  0.0 20.6 %copy-start = (bf16[128,8192]{1,0:T(8,128)(2,1)S(1)}, bf16[128,8192]{1,0:T(8,128)(2,1)}, u32[]{:S(2)}) copy-start(bf16[128,8192]{1,0:T(8,128)(2,1)} %param.10) | copy-start | bytes 6291460
  1.9 15.3 %all-to-all-start.1 = ((bf16[128,4,256]{0,2,1:T(8,128)(2,1)}), bf16[128,4,256]{0,2,1:T(8,128)(2,1)S(1)}, u32[]{:S(2)}, u32[]{:S(2)}) async-start(bf16[128,4,256]{0,2,1:T(8,128)(2,1)} %bitcast.2), calls=%async_computation.1 | async-start | bytes 524288 | tf_op jit(solution)/shard_map/all_to_all | solution.py:26
  17.2 10.4 %all-to-all-start.2 = ((bf16[128,4,256]{0,2,1:T(8,128)(2,1)}), bf16[128,4,256]{0,2,1:T(8,128)(2,1)S(1)}, u32[]{:S(2)}, u32[]{:S(2)}) async-start(bf16[128,4,256]{0,2,1:T(8,128)(2,1)} %bitcast.4), calls=%async_computation.2 | async-start | bytes 524288 | tf_op jit(solution)/shard_map/all_to_all | solution.py:27
  27.6 49.0 %all-to-all-start = ((bf16[128,4,2048]{2,0,1:T(8,128)(2,1)}), bf16[128,4,2048]{2,0,1:T(8,128)(2,1)S(1)}, u32[]{:S(2)}, u32[]{:S(2)}) async-start(bf16[128,4,2048]{2,0,1:T(8,128)(2,1)} %bitcast.143), calls=%async_computation | async-start | bytes 4194304 | tf_op jit(solution)/shard_map/all_to_all | solution.py:25
  31.2 17.2 %copy-start.3 = (s32[8]{0:T(128)S(1)}, s32[8]{0:T(128)}, u32[]{:S(2)}) copy-start(s32[8]{0:T(128)} %param.13) | copy-start | bytes 100
  31.6 11.6 %collective-permute-start = (bf16[2,512,256]{2,1,0:T(8,128)(2,1)S(1)}, bf16[2,512,256]{2,1,0:T(8,128)(2,1)}, u32[]{:S(2)}, u32[]{:S(2)}) collective-permute-start(bf16[2,512,256]{2,1,0:T(8,128)(2,1)S(1)} %pad_maximum_fusion), channel_id=1, source_target_pairs={{0,1},{1,2},{2,3},{3,4},{4,5},{5,6},{6,7},{8,9},{9,10},{10,11},{11... | collective-permute-start | bytes 1572872 | tf_op jit(solution)/shard_map/ppermute | solution.py:13
  43.2 13.9 %collective-permute-start.1 = (bf16[2,512,256]{2,1,0:T(8,128)(2,1)}, bf16[2,512,256]{2,1,0:T(8,128)(2,1)}, u32[]{:S(2)}, u32[]{:S(2)}) collective-permute-start(bf16[2,512,256]{2,1,0:T(8,128)(2,1)} %collective-permute-done), channel_id=1, source_target_pairs={{0,1},{1,2},{2,3},{3,4},{4,5},{5,6},{6,7},{8,9},{9,10},{10,11},{11... | collective-permute-start | bytes 1572872 | tf_op jit(solution)/shard_map/ppermute | solution.py:13
  80.5 1.0 copy-start.2
  83.8 1.0 copy-start.2
  87.2 1.0 copy-start.2
  90.5 1.0 copy-start.2
  93.9 1.0 copy-start.2
  97.2 1.0 copy-start.2
  100.6 1.0 copy-start.2
  103.9 1.0 copy-start.2
  107.2 2.4 copy-start.1
where the time goes:
time: 249 us; the launch traced here: 247 us
  matrix products  73 us (29%)
  blocking collectives  51 us (20%)
  waiting for transfers between devices  42.7 us (17%)
  local copies, waits for them, and re-layouts  30.7 us (12%)
  other arithmetic  25.2 us (10%)
  starting transfers between devices  22.9 us (9%)
    dot_general x24, matrix products, one_group(): jnp.einsum('kqc,ckd->qkd', weights.astype(jnp.bfloat16), value_heads, pre...  59.7 us
    all_to_all x1, blocking collectives, per_device(): lax.all_to_all(outcome, 'head', split_axis=0, concat_axis=1, tiled=True)  51 us
    all_to_all x1, waiting for transfers between devices, per_device(): lax.all_to_all(query, 'head', split_axis=1, concat_axis=0, tiled=True)  17.9 us
    reduce_sum x24, other arithmetic, one_group(): new_total = running_total * shrink + jnp.sum(weights, axis=2)  13.5 us
    dot_general x24, matrix products, one_group(): jnp.einsum('qkd,ckd->kqc', query_part, key_heads, preferred_element_type=...  13.3 us
    ppermute x2, waiting for transfers between devices, from_behind(): lax.ppermute(value, axis, [(source, source + steps) for source in range(l...  12.3 us
    ppermute x2, starting transfers between devices, from_behind(): lax.ppermute(value, axis, [(source, source + steps) for source in range(l...  9.49 us
    and x24, other arithmetic, attend(): (query_docs[:, None] == key_docs[None, :]) & (key_pos[None, :] <= query_p...  7.46 us
  transfers between devices with their start and end apart: 5, of which 5 were waited for; matrix products, arithmetic and copies ran while one was open for 4% of the time, Pallas kernels for 0%

commit v1 on v0

--- a/solution.py
+++ b/solution.py
@@ -1,3 +1,4 @@
+import functools
 import math
 import jax
 import jax.numpy as jnp
@@ -5,6 +6,21 @@
 from jax.sharding import PartitionSpec as P
 
 HEAD_SIZE = 128
+
+
+def put_keys_over_axis(own_rows, group_axis, axis_k, row_dim):
+    return jnp.concatenate(
+        lax.all_to_all(
+            jnp.stack(jnp.split(own_rows, lax.axis_size(group_axis), axis=axis_k), axis=0),
+            axis_name=group_axis,
+            split_axis=0,
+            concat_axis=0,
+        ),
+        axis=row_dim,
+    )
+
+
+_use_axis_part = functools.partial(put_keys_over_axis, group_axis="head", axis_k=0, row_dim=1)
 
 
 def from_behind(value, axis, steps):
@@ -87,7 +103,7 @@
     outcome = running_sum / jnp.transpose(running_total, (0, 2, 1))[..., None]
     outcome = jnp.transpose(outcome, (1, 2, 0, 3))
     outcome = outcome.reshape(local_len, pair_heads * group_width * HEAD_SIZE).astype(jnp.bfloat16)
-    return lax.all_to_all(outcome, "head", split_axis=0, concat_axis=1, tiled=True)
+    return _use_axis_part(outcome)
 
 
 def solution(mesh):

time: 249 us -> 269 us (1.080)
  matrix products: 73 us -> 89.4 us
  waiting for transfers between devices: 42.7 us -> 47.3 us
    dot_general x24, matrix products: 13.3 us -> 36 us  [one_group(): jnp.einsum('qkd,ckd->kqc', query_part, key_heads, preferred_element_type=...]
    dynamic_update_slice x0 -> x16, local copies, waits for them, and re-layouts: none -> 8.38 us  [attend(): return lax.map(one_group, (query_groups, state[0], state[1], state[2]))]
    dot_general x24, matrix products: 59.7 us -> 53.3 us  [one_group(): jnp.einsum('kqc,ckd->qkd', weights.astype(jnp.bfloat16), value_heads, pre...]
    all_to_all x2 -> x0, local copies, waits for them, and re-layouts: 5.92 us -> none  [per_device(): lax.all_to_all(outcome, 'head', split_axis=0, concat_axis=1, tiled=True)]
    convert_element_type x2 -> x0, local copies, waits for them, and re-layouts: 5.49 us -> none  [per_device(): outcome.reshape(local_len, pair_heads * group_width * HEAD_SIZE)]
    ppermute x2, waiting for transfers between devices: 12.3 us -> 16.1 us  [from_behind(): lax.ppermute(value, axis, [(source, source + steps) for source in range(l...]
    reshape x0 -> x1, local copies, waits for them, and re-layouts: none -> 2.88 us  [put_keys_over_axis(): jnp.concatenate(lax.all_to_all(jnp.stack(jnp.split(own_rows, lax.axis_siz...]
    another operation x8 -> x7, local copies, waits for them, and re-layouts: 7.23 us -> 4.87 us
  transfers between devices with their start and end apart: 5 -> 5, of which waited for: 5 -> 5; matrix products, arithmetic and copies ran while one was open for 4% -> 2% of each run, Pallas kernels for 0% -> 0%
where the time goes in v1:
time: 269 us; the launch traced here: 267 us
  matrix products  89.4 us (33%)
  blocking collectives  50.2 us (19%)
  waiting for transfers between devices  47.3 us (18%)
  local copies, waits for them, and re-layouts  31.4 us (12%)
  other arithmetic  25.4 us (9%)
  starting transfers between devices  22 us (8%)
    dot_general x24, matrix products, one_group(): jnp.einsum('kqc,ckd->qkd', weights.astype(jnp.bfloat16), value_heads, pre...  53.3 us
    all_to_all x1, blocking collectives, put_keys_over_axis(): lax.all_to_all(jnp.stack(jnp.split(own_rows, lax.axis_size(group_axis), a...  50.2 us
    dot_general x24, matrix products, one_group(): jnp.einsum('qkd,ckd->kqc', query_part, key_heads, preferred_element_type=...  36 us
    all_to_all x1, waiting for transfers between devices, per_device(): lax.all_to_all(query, 'head', split_axis=1, concat_axis=0, tiled=True)  18.5 us
    ppermute x2, waiting for transfers between devices, from_behind(): lax.ppermute(value, axis, [(source, source + steps) for source in range(l...  16.1 us
    reduce_sum x24, other arithmetic, one_group(): new_total = running_total * shrink + jnp.sum(weights, axis=2)  13.6 us
    unnamed x14, local copies, waits for them, and re-layouts  9.22 us
    dynamic_update_slice x16, local copies, waits for them, and re-layouts, attend(): return lax.map(one_group, (query_groups, state[0], state[1], state[2]))  8.38 us
  transfers between devices with their start and end apart: 5, of which 5 were waited for; matrix products, arithmetic and copies ran while one was open for 2% of the time, Pallas kernels for 0%

profile of v1, /device:TPU:0, one launch (start us, length us, event | category | flops | bytes accessed | tf_op | source)
XLA Modules:
  0.0 267.0 jit_solution(10690218235816409125)
XLA Ops:
  0.0 1.9 copy.58
  1.9 6.3 %all-to-all-start.1 = ((bf16[128,4,256]{0,2,1:T(8,128)(2,1)}), bf16[128,4,256]{0,2,1:T(8,128)(2,1)S(1)}, u32[]{:S(2)}, u32[]{:S(2)}) async-start(bf16[128,4,256]{0,2,1:T(8,128)(2,1)} %bitcast.2), calls=%async_computation.1 | async-start | bytes 524288 | tf_op jit(solution)/shard_map/all_to_all | solution.py:42
  8.3 1.8 copy.60
  10.1 7.1 %all-to-all-done.1 = bf16[128,4,256]{0,2,1:T(8,128)(2,1)S(1)} async-done(((bf16[128,4,256]{0,2,1:T(8,128)(2,1)}), bf16[128,4,256]{0,2,1:T(8,128)(2,1)S(1)}, u32[]{:S(2)}, u32[]{:S(2)}) %all-to-all-start.1) | async-done | bytes 262176 | tf_op jit(solution)/shard_map/all_to_all | solution.py:42
  17.2 3.4 %all-to-all-start.2 = ((bf16[128,4,256]{0,2,1:T(8,128)(2,1)}), bf16[128,4,256]{0,2,1:T(8,128)(2,1)S(1)}, u32[]{:S(2)}, u32[]{:S(2)}) async-start(bf16[128,4,256]{0,2,1:T(8,128)(2,1)} %bitcast.4), calls=%async_computation.2 | async-start | bytes 524288 | tf_op jit(solution)/shard_map/all_to_all | solution.py:43
  22.1 5.5 %all-to-all-done.2 = bf16[128,4,256]{0,2,1:T(8,128)(2,1)S(1)} async-done(((bf16[128,4,256]{0,2,1:T(8,128)(2,1)}), bf16[128,4,256]{0,2,1:T(8,128)(2,1)S(1)}, u32[]{:S(2)}, u32[]{:S(2)}) %all-to-all-start.2) | async-done | bytes 262176 | tf_op jit(solution)/shard_map/all_to_all | solution.py:43
  27.6 4.4 %all-to-all-start = ((bf16[128,4,2048]{2,0,1:T(8,128)(2,1)}), bf16[128,4,2048]{2,0,1:T(8,128)(2,1)}, u32[]{:S(2)}, u32[]{:S(2)}) async-start(bf16[128,4,2048]{2,0,1:T(8,128)(2,1)} %bitcast.142), calls=%async_computation | async-start | bytes 4194304 | tf_op jit(solution)/shard_map/all_to_all | solution.py:41
  32.4 3.4 %collective-permute-start = (bf16[2,512,256]{2,1,0:T(8,128)(2,1)S(1)}, bf16[2,512,256]{2,1,0:T(8,128)(2,1)S(1)}, u32[]{:S(2)}, u32[]{:S(2)}) collective-permute-start(bf16[2,512,256]{2,1,0:T(8,128)(2,1)S(1)} %pad_maximum_fusion.1), channel_id=1, source_target_pairs={{0,1},{1,2},{2,3},{3,4},{4,5},{5,6},{6,7},{8,9},{9,10},{10,11},{11... | collective-permute-start | bytes 1572872 | tf_op jit(solution)/shard_map/ppermute | solution.py:29
  35.9 8.1 %collective-permute-done = bf16[2,512,256]{2,1,0:T(8,128)(2,1)S(1)} collective-permute-done((bf16[2,512,256]{2,1,0:T(8,128)(2,1)S(1)}, bf16[2,512,256]{2,1,0:T(8,128)(2,1)S(1)}, u32[]{:S(2)}, u32[]{:S(2)}) %collective-permute-start) | collective-permute-done | bytes 524320 | tf_op jit(solution)/shard_map/ppermute | solution.py:29
  44.0 4.4 %collective-permute-start.1 = (bf16[2,512,256]{2,1,0:T(8,128)(2,1)S(1)}, bf16[2,512,256]{2,1,0:T(8,128)(2,1)S(1)}, u32[]{:S(2)}, u32[]{:S(2)}) collective-permute-start(bf16[2,512,256]{2,1,0:T(8,128)(2,1)S(1)} %collective-permute-done), channel_id=1, source_target_pairs={{0,1},{1,2},{2,3},{3,4},{4,5},{5,6},{6,7},{8,9},{9,10},{10,11},{11... | collective-permute-start | bytes 1572872 | tf_op jit(solution)/shard_map/ppermute | solution.py:29
  49.7 8.0 %collective-permute-done.1 = bf16[2,512,256]{2,1,0:T(8,128)(2,1)S(1)} collective-permute-done((bf16[2,512,256]{2,1,0:T(8,128)(2,1)S(1)}, bf16[2,512,256]{2,1,0:T(8,128)(2,1)S(1)}, u32[]{:S(2)}, u32[]{:S(2)}) %collective-permute-start.1) | collective-permute-done | bytes 524320 | tf_op jit(solution)/shard_map/ppermute | solution.py:29
  59.1 18.5 %all-to-all-done = bf16[128,4,2048]{2,0,1:T(8,128)(2,1)} async-done(((bf16[128,4,2048]{2,0,1:T(8,128)(2,1)}), bf16[128,4,2048]{2,0,1:T(8,128)(2,1)}, u32[]{:S(2)}, u32[]{:S(2)}) %all-to-all-start) | async-done | bytes 2097184 | tf_op jit(solution)/shard_map/all_to_all | solution.py:41
  77.6 2.2 copy.86
  79.8 1.9 copy.62
  81.7 2.4 broadcast.125.clone.1
  84.1 34.1 %while.43 = (s32[]{:T(128)}, f32[8,2,512]{2,1,0:T(2,128)S(1)}, f32[8,2,512]{2,1,0:T(2,128)S(1)}, f32[8,512,2,128]{3,1,2,0:T(8,128)}, bf16[8,512,2,128]{3,1,2,0:T...) while((s32[]{:T(128)}, f32[8,2,512]{2,1,0:T(2,128)S(1)}, ...), condition=%wide.region_5.6_spmd.clone, body=%wide.region_2.0_spmd.clone.sunk | while | flops 276435968 | bytes 8705649 | solution.py:89
  84.4 1.5 fusion.108
  86.0 1.8 fusion.111
  90.3 1.9 fusion.111
  94.6 1.8 fusion.111
  98.8 1.8 fusion.111
  103.0 1.8 fusion.111
  105.8 1.5 fusion.108
  107.3 1.8 fusion.111
  111.6 1.8 fusion.111
  115.8 1.8 fusion.111
  118.2 2.4 broadcast.125
  120.6 42.4 %while.44 = (s32[]{:T(128)}, f32[8,2,512]{2,1,0:T(2,128)S(1)}, f32[8,2,512]{2,1,0:T(2,128)S(1)}, f32[8,512,2,128]{3,1,2,0:T(8,128)}, f32[8,2,512]{2,1,0:T(2,128)...) while((s32[]{:T(128)}, f32[8,2,512]{2,1,0:T(2,128)S(1)}, ...), condition=%wide.region_10.11_spmd.clone, body=%wide.region_7.10_spmd.clone.sunk | while | flops 276566016 | bytes 9246365 | solution.py:89
  122.5 2.8 %fusion.119 = f32[8,512,2,128]{3,1,2,0:T(8,128)} fusion(f32[8,512,2,128]{3,1,2,0:T(8,128)} %get-tuple-element.811, s32[]{:T(128)} %get-tuple-element.808, bf16[512,2,128]{2,0,1:T(8,128)(2,1)S(1)} %get-tuple-element.833, f32[2,512,512]{1,2,0:T(8,128)S(1)} %get-tuple-element.735, f32[2,512]{1,0:T(2,128)S(1)} %get-tuple-element.737, ...), kind=kOutput, calls=%fused_computation.40.clone.1 | convolution fusion | flops 137101312 | bytes 3678720 | tf_op jit(solution)/shard_map/while/body/eval_jaxpr/kqc,ckd->qkd/dot_general | solution.py:80
  127.8 2.9 %fusion.119 = f32[8,512,2,128]{3,1,2,0:T(8,128)} fusion(f32[8,512,2,128]{3,1,2,0:T(8,128)} %get-tuple-element.811, s32[]{:T(128)} %get-tuple-element.808, bf16[512,2,128]{2,0,1:T(8,128)(2,1)S(1)} %get-tuple-element.833, f32[2,512,512]{1,2,0:T(8,128)S(1)} %get-tuple-element.735, f32[2,512]{1,0:T(2,128)S(1)} %get-tuple-element.737, ...), kind=kOutput, calls=%fused_computation.40.clone.1 | convolution fusion | flops 137101312 | bytes 3678720 | tf_op jit(solution)/shard_map/while/body/eval_jaxpr/kqc,ckd->qkd/dot_general | solution.py:80
  133.1 2.8 %fusion.119 = f32[8,512,2,128]{3,1,2,0:T(8,128)} fusion(f32[8,512,2,128]{3,1,2,0:T(8,128)} %get-tuple-element.811, s32[]{:T(128)} %get-tuple-element.808, bf16[512,2,128]{2,0,1:T(8,128)(2,1)S(1)} %get-tuple-element.833, f32[2,512,512]{1,2,0:T(8,128)S(1)} %get-tuple-element.735, f32[2,512]{1,0:T(2,128)S(1)} %get-tuple-element.737, ...), kind=kOutput, calls=%fused_computation.40.clone.1 | convolution fusion | flops 137101312 | bytes 3678720 | tf_op jit(solution)/shard_map/while/body/eval_jaxpr/kqc,ckd->qkd/dot_general | solution.py:80
  138.4 2.8 %fusion.119 = f32[8,512,2,128]{3,1,2,0:T(8,128)} fusion(f32[8,512,2,128]{3,1,2,0:T(8,128)} %get-tuple-element.811, s32[]{:T(128)} %get-tuple-element.808, bf16[512,2,128]{2,0,1:T(8,128)(2,1)S(1)} %get-tuple-element.833, f32[2,512,512]{1,2,0:T(8,128)S(1)} %get-tuple-element.735, f32[2,512]{1,0:T(2,128)S(1)} %get-tuple-element.737, ...), kind=kOutput, calls=%fused_computation.40.clone.1 | convolution fusion | flops 137101312 | bytes 3678720 | tf_op jit(solution)/shard_map/while/body/eval_jaxpr/kqc,ckd->qkd/dot_general | solution.py:80
  143.7 2.8 %fusion.119 = f32[8,512,2,128]{3,1,2,0:T(8,128)} fusion(f32[8,512,2,128]{3,1,2,0:T(8,128)} %get-tuple-element.811, s32[]{:T(128)} %get-tuple-element.808, bf16[512,2,128]{2,0,1:T(8,128)(2,1)S(1)} %get-tuple-element.833, f32[2,512,512]{1,2,0:T(8,128)S(1)} %get-tuple-element.735, f32[2,512]{1,0:T(2,128)S(1)} %get-tuple-element.737, ...), kind=kOutput, calls=%fused_computation.40.clone.1 | convolution fusion | flops 137101312 | bytes 3678720 | tf_op jit(solution)/shard_map/while/body/eval_jaxpr/kqc,ckd->qkd/dot_general | solution.py:80
  149.0 2.9 %fusion.119 = f32[8,512,2,128]{3,1,2,0:T(8,128)} fusion(f32[8,512,2,128]{3,1,2,0:T(8,128)} %get-tuple-element.811, s32[]{:T(128)} %get-tuple-element.808, bf16[512,2,128]{2,0,1:T(8,128)(2,1)S(1)} %get-tuple-element.833, f32[2,512,512]{1,2,0:T(8,128)S(1)} %get-tuple-element.735, f32[2,512]{1,0:T(2,128)S(1)} %get-tuple-element.737, ...), kind=kOutput, calls=%fused_computation.40.clone.1 | convolution fusion | flops 137101312 | bytes 3678720 | tf_op jit(solution)/shard_map/while/body/eval_jaxpr/kqc,ckd->qkd/dot_general | solution.py:80
  154.3 2.8 %fusion.119 = f32[8,512,2,128]{3,1,2,0:T(8,128)} fusion(f32[8,512,2,128]{3,1,2,0:T(8,128)} %get-tuple-element.811, s32[]{:T(128)} %get-tuple-element.808, bf16[512,2,128]{2,0,1:T(8,128)(2,1)S(1)} %get-tuple-element.833, f32[2,512,512]{1,2,0:T(8,128)S(1)} %get-tuple-element.735, f32[2,512]{1,0:T(2,128)S(1)} %get-tuple-element.737, ...), kind=kOutput, calls=%fused_computation.40.clone.1 | convolution fusion | flops 137101312 | bytes 3678720 | tf_op jit(solution)/shard_map/while/body/eval_jaxpr/kqc,ckd->qkd/dot_general | solution.py:80
  159.6 2.8 %fusion.119 = f32[8,512,2,128]{3,1,2,0:T(8,128)} fusion(f32[8,512,2,128]{3,1,2,0:T(8,128)} %get-tuple-element.811, s32[]{:T(128)} %get-tuple-element.808, bf16[512,2,128]{2,0,1:T(8,128)(2,1)S(1)} %get-tuple-element.833, f32[2,512,512]{1,2,0:T(8,128)S(1)} %get-tuple-element.735, f32[2,512]{1,0:T(2,128)S(1)} %get-tuple-element.737, ...), kind=kOutput, calls=%fused_computation.40.clone.1 | convolution fusion | flops 137101312 | bytes 3678720 | tf_op jit(solution)/shard_map/while/body/eval_jaxpr/kqc,ckd->qkd/dot_general | solution.py:80
  163.1 47.2 %while.45 = (s32[]{:T(128)}, f32[8,2,512]{2,1,0:T(2,128)S(1)}, f32[8,512,2,128]{1,3,0,2:T(8,128)}, f32[8,2,512]{2,1,0:T(2,128)S(1)}, f32[8,2,512]{2,1,0:T(2,128)...) while((s32[]{:T(128)}, f32[8,2,512]{2,1,0:T(2,128)S(1)}, ...), condition=%wide.region_15.16_spmd.clone, body=%wide.region_12.15_spmd.clone.sunk | while | flops 276566016 | bytes 14485229 | solution.py:89
  165.0 2.0 fusion.127
  170.9 2.0 fusion.127
  176.8 2.0 fusion.127
  182.7 2.0 fusion.127
  188.6 2.0 fusion.127
  194.4 2.0 fusion.127
  200.3 2.0 fusion.127
  206.2 2.0 fusion.127
  210.3 2.8 %fusion.72 = bf16[512,2,8,128]{0,3,2,1:T(8,128)(2,1)S(1)} fusion(f32[8,512,2,128]{1,3,0,2:T(8,128)} %get-tuple-element.167, f32[8,512,2]{1,0,2:T(8,128)S(1)} %copy.77), kind=kLoop, calls=%fused_computation.97 | loop fusion | flops 2097152 | bytes 6324224 | tf_op jit(solution)/shard_map/convert_element_type | solution.py:105
  214.0 50.2 %all_to_all.53 = bf16[4,128,2048]{1,2,0:T(8,128)(2,1)S(1)} all-to-all(bf16[4,128,2048]{1,2,0:T(8,128)(2,1)S(1)} %pad_maximum_fusion), channel_id=1, replica_groups=mesh['head'=4,'outer'=2,'inner'=4] {'head'}, dimensions={0} | all-to-all | bytes 4194304 | tf_op jit(solution)/shard_map/all_to_all | solution.py:13
  264.2 2.9 %copy.79 = bf16[128,8192]{1,0:T(8,128)(2,1)} copy(bf16[128,8192]{0,1:T(8,128)(2,1)S(1)} %bitcast.200) | data formatting | bytes 4194304 | tf_op jit(solution)/shard_map/reshape | solution.py:12
  (220 shorter events, 71.5 us)
Async XLA Ops:
  0.0 20.6 %copy-start.2 = (bf16[128,8192]{1,0:T(8,128)(2,1)S(1)}, bf16[128,8192]{1,0:T(8,128)(2,1)}, u32[]{:S(2)}) copy-start(bf16[128,8192]{1,0:T(8,128)(2,1)} %param.10) | copy-start | bytes 6291460
  1.9 15.3 %all-to-all-start.1 = ((bf16[128,4,256]{0,2,1:T(8,128)(2,1)}), bf16[128,4,256]{0,2,1:T(8,128)(2,1)S(1)}, u32[]{:S(2)}, u32[]{:S(2)}) async-start(bf16[128,4,256]{0,2,1:T(8,128)(2,1)} %bitcast.2), calls=%async_computation.1 | async-start | bytes 524288 | tf_op jit(solution)/shard_map/all_to_all | solution.py:42
  17.2 10.4 %all-to-all-start.2 = ((bf16[128,4,256]{0,2,1:T(8,128)(2,1)}), bf16[128,4,256]{0,2,1:T(8,128)(2,1)S(1)}, u32[]{:S(2)}, u32[]{:S(2)}) async-start(bf16[128,4,256]{0,2,1:T(8,128)(2,1)} %bitcast.4), calls=%async_computation.2 | async-start | bytes 524288 | tf_op jit(solution)/shard_map/all_to_all | solution.py:43
  27.6 50.0 %all-to-all-start = ((bf16[128,4,2048]{2,0,1:T(8,128)(2,1)}), bf16[128,4,2048]{2,0,1:T(8,128)(2,1)}, u32[]{:S(2)}, u32[]{:S(2)}) async-start(bf16[128,4,2048]{2,0,1:T(8,128)(2,1)} %bitcast.142), calls=%async_computation | async-start | bytes 4194304 | tf_op jit(solution)/shard_map/all_to_all | solution.py:41
  32.1 16.4 %copy-start.4 = (s32[8]{0:T(128)S(1)}, s32[8]{0:T(128)}, u32[]{:S(2)}) copy-start(s32[8]{0:T(128)} %param.13) | copy-start | bytes 100
  32.4 11.6 %collective-permute-start = (bf16[2,512,256]{2,1,0:T(8,128)(2,1)S(1)}, bf16[2,512,256]{2,1,0:T(8,128)(2,1)S(1)}, u32[]{:S(2)}, u32[]{:S(2)}) collective-permute-start(bf16[2,512,256]{2,1,0:T(8,128)(2,1)S(1)} %pad_maximum_fusion.1), channel_id=1, source_target_pairs={{0,1},{1,2},{2,3},{3,4},{4,5},{5,6},{6,7},{8,9},{9,10},{10,11},{11... | collective-permute-start | bytes 1572872 | tf_op jit(solution)/shard_map/ppermute | solution.py:29
  44.0 13.7 %collective-permute-start.1 = (bf16[2,512,256]{2,1,0:T(8,128)(2,1)S(1)}, bf16[2,512,256]{2,1,0:T(8,128)(2,1)S(1)}, u32[]{:S(2)}, u32[]{:S(2)}) collective-permute-start(bf16[2,512,256]{2,1,0:T(8,128)(2,1)S(1)} %collective-permute-done), channel_id=1, source_target_pairs={{0,1},{1,2},{2,3},{3,4},{4,5},{5,6},{6,7},{8,9},{9,10},{10,11},{11... | collective-permute-start | bytes 1572872 | tf_op jit(solution)/shard_map/ppermute | solution.py:29
  163.1 1.9 copy-start
  163.1 1.9 copy-start.3
  168.0 0.9 copy-start.1
  169.0 1.9 copy-start
  169.0 1.9 copy-start.3
  173.9 0.9 copy-start.1
  174.9 1.9 copy-start
  174.9 1.9 copy-start.3
  179.8 0.9 copy-start.1
  180.8 1.9 copy-start
  180.8 1.9 copy-start.3
  185.7 0.9 copy-start.1
  186.7 1.9 copy-start
  186.7 1.9 copy-start.3
  191.6 0.9 copy-start.1
  192.6 1.9 copy-start
  192.6 1.9 copy-start.3
  197.5 0.9 copy-start.1
  198.5 1.9 copy-start
  198.5 1.9 copy-start.3
  203.4 0.9 copy-start.1
  204.4 1.9 copy-start
  204.4 1.9 copy-start.3
  209.3 0.9 copy-start.1
